TPU v7x, 32 devices: a whole 2x2x4 slice. The times are simulated.
32 devices in a mesh: mem: 8 (over z, x), geo: 4 (over y, core).
Axes of the slice: x: 2, y: 2, z: 4, core: 2. Of those that a mesh axis runs over, the one named last changes fastest.
Arguments:
- control: float32 [8, 32, 48, 384], P('mem', 'geo'), may hold values from -6 to 6
- kappa_table: float32 [16], replicated, may hold values from 0.02 to 0.24
- kappa_index: int32 [48, 384], replicated, may hold values from 0 to 15
- tile_bounds: int32 [5], replicated, may hold values from 0 to 18432, as said below
- filter_bands: float32 [4, 5, 32], replicated, may hold values from -0.3 to 0.3
- perturbation: bfloat16 [2, 8, 32, 18432], P(None, 'mem', None, 'geo'), may hold values from -6 to 6
Outputs:
- increment: float32 [2, 32, 18432], P(None, 'mem', 'geo')
Inputs may be any that keep to these rules, and one draw needn't show every extreme that they name: tile_bounds[0] is 0, tile_bounds[4] is 18432, and the bounds never fall; tile t holds columns tile_bounds[t] to tile_bounds[t + 1] - 1.
All inputs are finite; a program needn't handle non-finite values.
Results may differ from a plain program's by a relative error of at most 0.005.
Values may be sent and summed in bfloat16 or wider, within the bound.
A program may use at most 64 MiB of HBM per device.

v0:
```python
import jax
import jax.numpy as jnp
from jax import lax
from jax.sharding import PartitionSpec as P

ITERS = 10


def neighbours(state):
    east = jnp.concatenate([state[..., 1:, :], state[..., -1:, :]], axis=-2)
    west = jnp.concatenate([state[..., :1, :], state[..., :-1, :]], axis=-2)
    north = jnp.concatenate([state[..., 1:], state[..., -1:]], axis=-1)
    south = jnp.concatenate([state[..., :1], state[..., :-1]], axis=-1)
    return (east, west, north, south)


def face_weights(kappa_field):
    return tuple((0.5 * (kappa_field + other) for other in neighbours(kappa_field)))


def diffuse_step(state, weights):
    east, west, north, south = neighbours(state)
    update = weights[0] * (east - state) + weights[1] * (west - state)
    update = update + weights[2] * (north - state) + weights[3] * (south - state)
    return state + update


def vertical_filter(values, coefficients):
    levels = values.shape[0]
    padded = jnp.pad(values, ((2, 2), (0, 0)))
    result = values
    for offset in range(5):
        result = result + coefficients[offset] * padded[offset : offset + levels]
    return result


def body(control, kappa_table, kappa_index, tile_bounds, filter_bands, perturbation):
    moved_pert = lax.all_to_all(perturbation, "mem", split_axis=2, concat_axis=1, tiled=True)
    kappa_field = jnp.zeros(kappa_index.shape, jnp.float32)
    for entry in range(kappa_table.shape[0]):
        kappa_field = kappa_field + jnp.where(kappa_index == entry, kappa_table[entry], 0.0)
    weights = face_weights(kappa_field)
    state_field = lax.fori_loop(0, ITERS, lambda step, cur: diffuse_step(cur, weights), control)
    flattened = state_field.reshape(state_field.shape[0], state_field.shape[1], -1)
    by_columns = lax.all_to_all(flattened, "geo", split_axis=2, concat_axis=1, tiled=True)
    width = by_columns.shape[2]
    tiles_count = filter_bands.shape[0]
    columns = lax.axis_index("geo") * width + jnp.arange(width, dtype=jnp.int32)
    tile_ids = jnp.sum((columns[None, :] >= tile_bounds[1:-1][:, None]).astype(jnp.int32), axis=0)
    one_hot = (tile_ids[None, :] == jnp.arange(tiles_count, dtype=jnp.int32)[:, None]).astype(
        jnp.float32
    )
    coefficients = jnp.einsum("tkl,tc->klc", filter_bands, one_hot, precision=lax.Precision.HIGHEST)
    filtered = vertical_filter(by_columns[0], coefficients).astype(jnp.bfloat16)
    moved_filtered = lax.all_to_all(filtered[None], "mem", split_axis=1, concat_axis=0, tiled=True)
    return jnp.sum(
        moved_pert.astype(jnp.float32) * moved_filtered.astype(jnp.float32)[None], axis=1
    )


def solution(mesh):
    in_specs = (P("mem", "geo", None, None), P(), P(), P(), P(), P(None, "mem", None, "geo"))
    out_specs = P(None, "mem", "geo")
    return jax.shard_map(body, mesh=mesh, in_specs=in_specs, out_specs=out_specs, check_vma=False)
```

profile of v0, /device:TPU:0, one launch (start us, length us, event | category | flops | bytes accessed | tf_op | source)
XLA Modules:
  0.0 219.2 jit_solution(1623861114880907975)
XLA Ops:
  0.0 1.1 copy.36
  1.1 1.9 fusion.36
  3.0 10.8 %select_add_fusion = f32[48,384]{1,0:T(8,128)S(1)} fusion(s32[48,384]{1,0:T(8,128)} %param.10, f32[]{:T(128)} %bitcast.16, f32[]{:T(128)} %bitcast.15, f32[]{:T(128)} %bitcast.14, f32[]{:T(128)} %bitcast.13, f32[]{:T(128)} %bitcast.12, f32[]{:T(128)} %bitcast.11, f32[]{:T(128)} %bitcast.10, f32[]{:T(128)} %bitcast.9, f32[]{:T(128)} %bitcast.8, f32[]{:T(128)} %bitcast.7, ...), kind=kLoop, calls=%fused_computation.47 | loop fusion | flops 866304 | bytes 147520 | tf_op jit(solution)/shard_map/add | solution.py:41
  14.1 10.9 %fusion.24 = (f32[48,384]{1,0:T(8,128)S(1)}, f32[48,384]{1,0:T(8,128)S(1)}, f32[48,384]{1,0:T(8,128)S(1)}, f32[48,384]{1,0:T(8,128)S(1)}) fusion(f32[48,383]{1,0:T(8,128)S(1)} %get-tuple-element.64, f32[48,1]{1,0:T(8,128)S(1)} %get-tuple-element.62, f32[48,1]{1,0:T(8,128)S(1)} %get-tuple-element.63, f32[48,383]{1,0:T(8,128)S(1)} %get-tuple-element.65, ...), kind=kLoop, calls=%fused_computation.44 | loop fusion | flops 1087488 | bytes 663616 | tf_op jit(solution)/shard_map/mul | solution.py:18
  24.9 10.2 %while.10 = (s32[]{:T(128)}, f32[1,8,48,384]{3,2,1,0:T(8,128)S(1)}, f32[48,384]{1,0:T(8,128)S(1)}, f32[48,384]{1,0:T(8,128)S(1)}, f32[48,384]{1,0:T(8,128)S(1)}, /*index=5*/f32[48,384]{1,0:T(8,128)S(1)}, s32[]{:T(128)}) while((s32[]{:T(128)}, f32[1,8,48,384]{3,2,1,0:T(8,128)S(1)}, f32[48,384]{1,0:T(8,128)S(1)}, f32[48,384]{1,0:T(8,128)S(1)}, ...), condition=%wide.region_1.2_spmd, body=%wide.region_0.1_spmd.sunk | while | flops 2359298 | bytes 8552525 | solution.py:43
  25.4 0.6 fusion.47
  26.4 0.6 fusion.47
  27.4 0.6 fusion.47
  28.5 0.6 fusion.47
  29.5 0.6 fusion.47
  30.5 0.6 fusion.47
  31.5 0.6 fusion.47
  32.5 0.6 fusion.47
  35.2 5.5 %copy.21 = f32[1,8,48,384]{1,3,2,0:T(8,128)} copy(f32[1,8,48,384]{3,2,1,0:T(8,128)S(1)} %get-tuple-element.37) | data formatting | bytes 1179648 | tf_op jit(solution)/shard_map/while | solution.py:43
  41.2 83.6 %reduce.2 = f32[18432,8]{1,0:T(8,128)} reduce(f32[18432,1,8]{2,1,0:T(1,128)} %bitcast.70, f32[]{:T(128)} %broadcast.28), dimensions={1}, to_apply=%bitcast.62.reduce_sub_computation | reduce | bytes 1179652
  124.8 7.8 %reshape.43 = f32[4,1,36864]{2,1,0:T(1,128)} reshape(f32[18432,8]{1,0:T(8,128)} %reduce.2) | data formatting | bytes 1179648
  132.6 4.3 %all-to-all-start.1 = ((f32[4,1,36864]{2,1,0:T(1,128)}), f32[4,1,36864]{2,1,0:T(1,128)}, u32[]{:S(2)}, u32[]{:S(2)}) async-start(f32[4,1,36864]{2,1,0:T(1,128)} %reshape.43), calls=%async_computation.1 | async-start | bytes 1179648 | tf_op jit(solution)/shard_map/all_to_all | solution.py:45
  137.2 1.3 convolution_bitcast_fusion
  138.5 8.5 %all-to-all-done.1 = f32[4,1,36864]{2,1,0:T(1,128)} async-done(((f32[4,1,36864]{2,1,0:T(1,128)}), f32[4,1,36864]{2,1,0:T(1,128)}, u32[]{:S(2)}, u32[]{:S(2)}) %all-to-all-start.1) | async-done | bytes 589856 | tf_op jit(solution)/shard_map/all_to_all | solution.py:45
  147.0 3.3 %reduce.3 = f32[4,36864]{1,0:T(4,128)S(1)} reduce(f32[4,1,36864]{2,1,0:T(1,128)} %all-to-all-done.1, f32[]{:T(128)} %broadcast.28), dimensions={1}, to_apply=%all_to_all.11.reduce_sub_computation | reduce | bytes 1179652 | tf_op jit(solution)/shard_map/all_to_all | solution.py:45
  150.3 22.3 %reshape.44 = f32[18432,1,8]{2,1,0:T(1,128)} reshape(f32[4,36864]{1,0:T(4,128)S(1)} %reduce.3) | data formatting | bytes 1179648
  172.6 5.5 %copy.22 = f32[1,8,4,4608]{3,1,2,0:T(8,128)S(1)} copy(f32[1,8,4,4608]{1,3,2,0:T(8,128)} %bitcast.71) | data formatting | bytes 1179648 | tf_op jit(solution)/shard_map/all_to_all | solution.py:45
  179.5 2.5 %reduce.4 = bf16[32,4608]{1,0:T(8,128)(2,1)S(1)} reduce(bf16[32,1,4608]{2,1,0:T(2,128)(2,1)S(1)} %bitcast.72, bf16[]{:T(256)} %broadcast.30), dimensions={1}, to_apply=%bitcast.69.reduce_sub_computation | reduce | bytes 589826
  181.9 0.9 reshape.45
  182.8 6.6 %all-to-all-start.2 = ((bf16[8,2,9216]{2,1,0:T(2,128)(2,1)}), bf16[8,2,9216]{2,1,0:T(2,128)(2,1)S(1)}, u32[]{:S(2)}, u32[]{:S(2)}) async-start(bf16[8,2,9216]{2,1,0:T(2,128)(2,1)} %reshape.45), calls=%async_computation.2 | async-start | bytes 589824 | tf_op jit(solution)/shard_map/all_to_all | solution.py:55
  189.4 1.4 copy.20
  190.8 7.9 %all-to-all-done.2 = bf16[8,2,9216]{2,1,0:T(2,128)(2,1)S(1)} async-done(((bf16[8,2,9216]{2,1,0:T(2,128)(2,1)}), bf16[8,2,9216]{2,1,0:T(2,128)(2,1)S(1)}, u32[]{:S(2)}, u32[]{:S(2)}) %all-to-all-start.2) | async-done | bytes 294944 | tf_op jit(solution)/shard_map/all_to_all | solution.py:55
  198.7 3.6 %all-to-all-start = ((bf16[2,1,32,4608]{3,0,1,2:T(2,128)(2,1)}), bf16[2,1,32,4608]{3,0,1,2:T(2,128)(2,1)S(1)}, u32[]{:S(2)}, u32[]{:S(2)}) async-start(bf16[2,1,32,4608]{3,0,1,2:T(2,128)(2,1)} %copy.20), calls=%async_computation | async-start | bytes 1179648 | tf_op jit(solution)/shard_map/all_to_all | solution.py:38
  202.6 1.7 convert_reduce_fusion
  204.5 13.4 %all-to-all-done = bf16[2,1,32,4608]{3,0,1,2:T(2,128)(2,1)S(1)} async-done(((bf16[2,1,32,4608]{3,0,1,2:T(2,128)(2,1)}), bf16[2,1,32,4608]{3,0,1,2:T(2,128)(2,1)S(1)}, u32[]{:S(2)}, u32[]{:S(2)}) %all-to-all-start) | async-done | bytes 589856 | tf_op jit(solution)/shard_map/all_to_all | solution.py:38
  217.9 0.6 fusion.8
  218.5 0.7 copy.24
  (61 shorter events, 8.0 us)
Async XLA Ops:
  0.0 137.2 %copy-start = (f32[4,5,32]{2,0,1:T(4,128)S(1)}, f32[4,5,32]{2,0,1:T(4,128)}, u32[]{:S(2)}) copy-start(f32[4,5,32]{2,0,1:T(4,128)} %param.12) | copy-start | bytes 7684
  124.8 12.2 %copy-start.2 = (s32[5]{0:T(128)S(1)}, s32[5]{0:T(128)}, u32[]{:S(2)}) copy-start(s32[5]{0:T(128)} %param.11) | copy-start | bytes 64
  132.6 14.4 %all-to-all-start.1 = ((f32[4,1,36864]{2,1,0:T(1,128)}), f32[4,1,36864]{2,1,0:T(1,128)}, u32[]{:S(2)}, u32[]{:S(2)}) async-start(f32[4,1,36864]{2,1,0:T(1,128)} %reshape.43), calls=%async_computation.1 | async-start | bytes 1179648 | tf_op jit(solution)/shard_map/all_to_all | solution.py:45
  178.5 10.9 %copy-start.1 = (bf16[2,1,32,4608]{3,2,1,0:T(8,128)(2,1)S(1)}, bf16[2,1,32,4608]{3,2,1,0:T(8,128)(2,1)}, u32[]{:S(2)}) copy-start(bf16[2,1,32,4608]{3,2,1,0:T(8,128)(2,1)} %param.13) | copy-start | bytes 1769476
  182.8 15.8 %all-to-all-start.2 = ((bf16[8,2,9216]{2,1,0:T(2,128)(2,1)}), bf16[8,2,9216]{2,1,0:T(2,128)(2,1)S(1)}, u32[]{:S(2)}, u32[]{:S(2)}) async-start(bf16[8,2,9216]{2,1,0:T(2,128)(2,1)} %reshape.45), calls=%async_computation.2 | async-start | bytes 589824 | tf_op jit(solution)/shard_map/all_to_all | solution.py:55
  198.7 19.2 %all-to-all-start = ((bf16[2,1,32,4608]{3,0,1,2:T(2,128)(2,1)}), bf16[2,1,32,4608]{3,0,1,2:T(2,128)(2,1)S(1)}, u32[]{:S(2)}, u32[]{:S(2)}) async-start(bf16[2,1,32,4608]{3,0,1,2:T(2,128)(2,1)} %copy.20), calls=%async_computation | async-start | bytes 1179648 | tf_op jit(solution)/shard_map/all_to_all | solution.py:38
where the time goes:
time: 220 us; the launch traced here: 219 us
  other arithmetic  119 us (54%)
  local copies, waits for them, and re-layouts  53.6 us (24%)
  waiting for transfers between devices  29.8 us (14%)
  starting transfers between devices  14.5 us (7%)
    unnamed x2, other arithmetic  86 us
    unnamed x14, local copies, waits for them, and re-layouts  34.8 us
    all_to_all x1, waiting for transfers between devices, body(): lax.all_to_all(perturbation, 'mem', split_axis=2, concat_axis=1, tiled=True)  13.4 us
    mul x1, other arithmetic, face_weights(): 0.5 * (kappa_field + other)  10.9 us
    add x1, other arithmetic, body(): kappa_field + jnp.where(kappa_index == entry, kappa_table[entry], 0.0)  10.8 us
    all_to_all x1, waiting for transfers between devices, body(): lax.all_to_all(flattened, 'geo', split_axis=2, concat_axis=1, tiled=True)  8.52 us
    all_to_all x1, waiting for transfers between devices, body(): lax.all_to_all(filtered[None], 'mem', split_axis=1, concat_axis=0, tiled=...  7.85 us
    all_to_all x1, starting transfers between devices, body(): lax.all_to_all(filtered[None], 'mem', split_axis=1, concat_axis=0, tiled=...  6.57 us
  transfers between devices with their start and end apart: 3, of which 3 were waited for; matrix products, arithmetic and copies ran while one was open for 2% of the time, Pallas kernels for 0%

commit v1 on v0

v1 whole, which is shorter than its diff:
```python
import functools

import jax
import jax.numpy as jnp
from jax import lax
from jax.experimental import pallas as pl
from jax.experimental.pallas import tpu as pltpu
from jax.sharding import PartitionSpec as P

ITERS = 10
F32, BF16 = jnp.float32, jnp.bfloat16
LANES = 128


def kernel(nm, ng, ctrl, table, kidx_hbm, bounds, bands_hbm, pert_hbm, out,
           S, WE, WN, kidx, kf, bands, bandsb, coef, pert, PS, PR, B, G, D, FS, FR,
           loc_sem, ps_sem, pr_sem, gs_sem, gr_sem, fs_sem, fr_sem):
    mem = lax.axis_index("mem")
    geo = lax.axis_index("geo")
    hx, lev, hy = S.shape
    nvar, levels, cols = pert.shape
    lm = levels // nm
    rows = hx // ng
    tiles, nband, _ = bands.shape
    pad = nband // 2

    barrier = pltpu.get_barrier_semaphore()
    for d in range(1, nm):
        pl.semaphore_signal(barrier, inc=1, device_id={"mem": lax.rem(mem + d, nm)}, device_id_type=pl.DeviceIdType.MESH)
    for d in range(1, ng):
        pl.semaphore_signal(barrier, inc=1, device_id={"geo": lax.rem(geo + d, ng)}, device_id_type=pl.DeviceIdType.MESH)

    pert_cp = pltpu.make_async_copy(pert_hbm.at[:, 0], pert, loc_sem.at[0])
    pert_cp.start()
    kidx_cp = pltpu.make_async_copy(kidx_hbm, kidx, loc_sem.at[1])
    kidx_cp.start()
    bands_cp = pltpu.make_async_copy(bands_hbm, bands, loc_sem.at[2])
    bands_cp.start()
    ctrl_cps = []
    for l in range(lev):
        cp = pltpu.make_async_copy(ctrl.at[0, l], S.at[:, l], loc_sem.at[3 + l])
        cp.start()
        ctrl_cps.append(cp)

    pert_cp.wait()

    def repack(q, carry):
        at = pl.ds(pl.multiple_of(q * LANES, LANES), LANES)
        vals = [pert[v, :, at].astype(F32) for v in range(nvar)]
        for m in range(nm):
            piece = jnp.concatenate([v[m * lm:(m + 1) * lm] for v in vals], axis=0)
            PS[m, :, at] = piece.astype(BF16)
        return carry

    lax.fori_loop(0, cols // LANES, repack, 0)
    pl.semaphore_wait(barrier, nm - 1 + ng - 1)

    def exchange(src, dst, send, recv, axis, me, d, n):
        peer = lax.rem(me + d, n)
        return pltpu.make_async_remote_copy(
            src_ref=src(peer), dst_ref=dst, send_sem=send.at[d], recv_sem=recv.at[d],
            device_id={axis: peer}, device_id_type=pl.DeviceIdType.MESH)

    pert_ex = [exchange(lambda p: PS.at[p], PR.at[d], ps_sem, pr_sem, "mem", mem, d, nm) for d in range(1, nm)]
    for cp in pert_ex:
        cp.start()

    kidx_cp.wait()
    index = kidx[...]
    field = jnp.zeros(index.shape, F32)
    for entry in range(table.shape[0]):
        field = jnp.where(index == entry, table[entry], field)
    kf[...] = field
    inner = lax.broadcasted_iota(jnp.int32, (1, hy), 1) < hy - 1

    def weights(i, carry):
        own = kf[pl.ds(i, 1), :]
        after = kf[pl.ds(jnp.minimum(i + 1, hx - 1), 1), :]
        WE[i] = jnp.broadcast_to(0.5 * (own + after), (lev, hy))
        north = jnp.where(inner, 0.5 * (own + pltpu.roll(own, hy - 1, axis=1)), 0.0)
        WN[i] = jnp.broadcast_to(north, (lev, hy))
        return carry

    lax.fori_loop(0, hx, weights, 0)

    def sweep(write):
        s, before = S[0], None
        for i in range(hx):
            fn = WN[i] * (pltpu.roll(s, hy - 1, axis=1) - s)
            new = s + (fn - pltpu.roll(fn, 1, axis=1))
            if before is not None:
                new = new - before
            if i < hx - 1:
                after = S[i + 1]
                before = WE[i] * (after - s)
                new = new + before
                s = after
            write(i, new)

    def keep(i, new):
        S[i] = new

    def narrow(i, new):
        B[i] = new.astype(BF16)

    for cp in ctrl_cps:
        cp.wait()

    def step(it, carry):
        sweep(keep)
        return carry

    lax.fori_loop(0, ITERS - 1, step, 0)
    sweep(narrow)

    geo_ex = [exchange(lambda p: B.at[pl.ds(p * rows, rows)], G.at[geo], gs_sem, gr_sem, "geo", geo, d, ng)
              for d in range(1, ng)]
    for cp in geo_ex:
        cp.start()
    own_geo = pltpu.make_async_copy(B.at[pl.ds(geo * rows, rows)], G.at[geo], gr_sem.at[0])
    own_geo.start()

    bands_cp.wait()
    eye = (lax.broadcasted_iota(jnp.int32, (levels, levels), 0)
           == lax.broadcasted_iota(jnp.int32, (levels, levels), 1))
    for t in range(tiles):
        for k in range(nband):
            row = jnp.broadcast_to(bands[t, k:k + 1, :], (levels, levels))
            column = jnp.sum(jnp.where(eye, row, 0.0), axis=1, keepdims=True)
            bandsb[t, k] = jnp.broadcast_to(column, (levels, LANES))

    def coefficients(q, carry):
        at = pl.ds(pl.multiple_of(q * LANES, LANES), LANES)
        column = geo * cols + q * LANES + lax.broadcasted_iota(jnp.int32, (levels, LANES), 1)
        past = [column >= bounds[t] for t in range(1, tiles)]
        for k in range(nband):
            value = bandsb[0, k]
            for t in range(1, tiles):
                value = jnp.where(past[t - 1], bandsb[t, k], value)
            coef[k, :, at] = value
        return carry

    lax.fori_loop(0, cols // LANES, coefficients, 0)
    base = 8
    D[0:base, :] = jnp.zeros((base, cols), F32)
    D[base + levels:, :] = jnp.zeros((D.shape[0] - base - levels, cols), F32)

    own_geo.wait()
    for cp in geo_ex:
        cp.wait_recv()
    for g in range(ng):
        for r in range(rows):
            D[base + g * lev:base + (g + 1) * lev, r * hy:(r + 1) * hy] = G[g, r].astype(F32)

    def vertical(q, carry):
        at = pl.ds(pl.multiple_of(q * LANES, LANES), LANES)
        value = D[base:base + levels, at]
        for k in range(nband):
            value = value + coef[k, :, at] * D[base + k - pad:base + k - pad + levels, at]
        for m in range(nm):
            FS[m, :, at] = value[m * lm:(m + 1) * lm].astype(BF16)
        return carry

    lax.fori_loop(0, cols // LANES, vertical, 0)
    filt_ex = [exchange(lambda p: FS.at[p], FR.at[d], fs_sem, fr_sem, "mem", mem, d, nm) for d in range(1, nm)]
    for cp in filt_ex:
        cp.start()
    own_filt = pltpu.make_async_copy(FS.at[mem], FR.at[0], fr_sem.at[0])
    own_filt.start()
    own_pert = pltpu.make_async_copy(PS.at[mem], PR.at[0], pr_sem.at[0])
    own_pert.start()
    own_pert.wait()
    own_filt.wait()
    for cp in pert_ex:
        cp.wait_recv()
    for cp in filt_ex:
        cp.wait_recv()

    def total(q, carry):
        at = pl.ds(pl.multiple_of(q * LANES, LANES), LANES)
        acc = jnp.zeros((nvar * lm, LANES), F32)
        for m in range(nm):
            f = FR[m, :, at].astype(F32)
            acc = acc + PR[m, :, at].astype(F32) * jnp.concatenate([f] * nvar, axis=0)
        for v in range(nvar):
            out[v, :, at] = acc[v * lm:(v + 1) * lm]
        return carry

    lax.fori_loop(0, cols // LANES, total, 0)
    for cp in pert_ex + geo_ex + filt_ex:
        cp.wait_send()


def body(nm, ng, control, kappa_table, kappa_index, tile_bounds, filter_bands, perturbation):
    _, lev, hx, hy = control.shape
    nvar, _, levels, cols = perturbation.shape
    lm = levels // nm
    rows = hx // ng
    tiles, nband, _ = filter_bands.shape
    dma = pltpu.SemaphoreType.DMA
    hbm = pl.BlockSpec(memory_space=pl.ANY)
    smem = pl.BlockSpec(memory_space=pltpu.SMEM)
    return pl.pallas_call(
        functools.partial(kernel, nm, ng),
        out_shape=jax.ShapeDtypeStruct((nvar, lm, cols), F32),
        in_specs=[hbm, smem, hbm, smem, hbm, hbm],
        out_specs=pl.BlockSpec(memory_space=pltpu.VMEM),
        scratch_shapes=[
            pltpu.VMEM((hx, lev, hy), F32),
            pltpu.VMEM((hx, lev, hy), F32),
            pltpu.VMEM((hx, lev, hy), F32),
            pltpu.VMEM((hx, hy), jnp.int32),
            pltpu.VMEM((hx, hy), F32),
            pltpu.VMEM((tiles, nband, levels), F32),
            pltpu.VMEM((tiles, nband, levels, LANES), F32),
            pltpu.VMEM((nband, levels, cols), F32),
            pltpu.VMEM((nvar, levels, cols), BF16),
            pltpu.VMEM((nm, nvar * lm, cols), BF16),
            pltpu.VMEM((nm, nvar * lm, cols), BF16),
            pltpu.VMEM((hx, lev, hy), BF16),
            pltpu.VMEM((ng, rows, lev, hy), BF16),
            pltpu.VMEM((levels + 16, cols), F32),
            pltpu.VMEM((nm, lm, cols), BF16),
            pltpu.VMEM((nm, lm, cols), BF16),
            dma((3 + lev,)), dma((nm,)), dma((nm,)), dma((ng,)), dma((ng,)), dma((nm,)), dma((nm,)),
        ],
        compiler_params=pltpu.CompilerParams(
            collective_id=0, has_side_effects=True, vmem_limit_bytes=56 * 2**20),
    )(control, kappa_table, kappa_index, tile_bounds, filter_bands, perturbation)


def solution(mesh):
    in_specs = (P("mem", "geo", None, None), P(), P(), P(), P(), P(None, "mem", None, "geo"))
    out_specs = P(None, "mem", "geo")
    run = functools.partial(body, mesh.shape["mem"], mesh.shape["geo"])
    return jax.shard_map(run, mesh=mesh, in_specs=in_specs, out_specs=out_specs, check_vma=False)
```

time: 220 us -> 48.3 us (0.22)
  other arithmetic: 119 us -> 0 us
  local copies, waits for them, and re-layouts: 53.6 us -> 2.89 us
  Pallas kernels: 0 us -> 45.2 us
  waiting for transfers between devices: 29.8 us -> 0 us
  starting transfers between devices: 14.5 us -> 0 us
    unnamed x2 -> x0, other arithmetic: 86 us -> none
    pallas_call x0 -> x1, Pallas kernels: none -> 45.2 us  [body(): pl.pallas_call(functools.partial(kernel, nm, ng), out_shape=jax.ShapeDtyp...]
    unnamed x14 -> x2, local copies, waits for them, and re-layouts: 34.8 us -> 2.89 us
    all_to_all x3 -> x0, waiting for transfers between devices: 29.8 us -> none  [the longest x1 13.4 us: body(): lax.all_to_all(perturbation, 'mem', split_axis=2, concat_axis=1, tiled=True)]
    add x12 -> x0, other arithmetic: 16.4 us -> none  [the longest x1 10.8 us: body(): kappa_field + jnp.where(kappa_index == entry, kappa_table[entry], 0.0)]
    all_to_all x3 -> x0, starting transfers between devices: 14.5 us -> none  [the longest x1 6.57 us: body(): lax.all_to_all(filtered[None], 'mem', split_axis=1, concat_axis=0, tiled=...]
    mul x1 -> x0, other arithmetic: 10.9 us -> none  [face_weights(): 0.5 * (kappa_field + other)]
    slice x46 -> x0, local copies, waits for them, and re-layouts: 6.46 us -> none  [the longest x22 3.44 us: neighbours(): south = jnp.concatenate([state[..., :1], state[..., :-1]], axis=-1)]
  transfers between devices with their start and end apart: 3 -> 0, of which waited for: 3 -> 0; matrix products, arithmetic and copies ran while one was open for 2% -> 0% of each run, Pallas kernels for 0% -> 0%
where the time goes in v1:
time: 48.3 us; the launch traced here: 48.1 us
  Pallas kernels  45.2 us (94%)
  local copies, waits for them, and re-layouts  2.89 us (6%)
    pallas_call x1, Pallas kernels, body(): pl.pallas_call(functools.partial(kernel, nm, ng), out_shape=jax.ShapeDtyp...  45.2 us
    unnamed x2, local copies, waits for them, and re-layouts  2.89 us

profile of v1, /device:TPU:0, one launch (start us, length us, event | category | flops | bytes accessed | tf_op | source)
XLA Modules:
  0.0 48.1 jit_solution(4373434951939556082)
XLA Ops:
  0.0 1.3 %copy.7.bands_hbm = f32[4,5,32]{2,1,0:T(8,128)} copy(f32[4,5,32]{2,0,1:T(4,128)} %param.10) | data formatting | bytes 5120 | tf_op args[4]
  1.3 45.2 %shard_map.64 = f32[2,4,4608]{2,1,0:T(4,128)} custom-call(f32[1,8,48,384]{3,2,1,0:T(8,128)} %ctrl.1, f32[16]{0:T(128)} %table.1, s32[48,384]{1,0:T(8,128)} %kidx_hbm.1, s32[5]{0:T(128)} %bounds.1, f32[4,5,32]{2,1,0:T(8,128)} %copy.7.bands_hbm, bf16[2,1,32,4608]{3,2,1,0:T(8,128)(2,1)} %pert_hbm.1), custom_call_target="tpu_custom_call" | custom-call | tf_op jit(solution)/shard_map/pallas_call | solution.py:203
  46.5 1.6 %copy.9 = f32[2,4,4608]{2,1,0:T(4,128)} copy(f32[2,4,4608]{2,1,0:T(4,128)} %shard_map.64) | data formatting | bytes 294912

commit v2 on v1

--- a/solution.py
+++ b/solution.py
@@ -12,8 +12,8 @@
 LANES = 128
 
 
-def kernel(nm, ng, ctrl, table, kidx_hbm, bounds, bands_hbm, pert_hbm, out,
-           S, WE, WN, kidx, kf, bands, bandsb, coef, pert, PS, PR, B, G, D, FS, FR,
+def kernel(nm, ng, ctrl, table_hbm, kidx_hbm, bounds_hbm, bands_hbm, pert_hbm, out,
+           table, bounds, S, WE, WN, WS, spread, gather, kidx, kf, bands, bandsb, coef, pert, PS, PR, B, G, D, FS, FR,
            loc_sem, ps_sem, pr_sem, gs_sem, gr_sem, fs_sem, fr_sem):
     mem = lax.axis_index("mem")
     geo = lax.axis_index("geo")
@@ -21,7 +21,8 @@
     nvar, levels, cols = pert.shape
     lm = levels // nm
     rows = hx // ng
-    tiles, nband, _ = bands.shape
+    nband, tiles, _ = bands.shape
+    parts = hy // LANES
     pad = nband // 2
 
     barrier = pltpu.get_barrier_semaphore()
@@ -36,23 +37,32 @@
     kidx_cp.start()
     bands_cp = pltpu.make_async_copy(bands_hbm, bands, loc_sem.at[2])
     bands_cp.start()
+    table_cp = pltpu.make_async_copy(table_hbm, table, loc_sem.at[3])
+    table_cp.start()
+    bounds_cp = pltpu.make_async_copy(bounds_hbm, bounds, loc_sem.at[4])
+    bounds_cp.start()
     ctrl_cps = []
     for l in range(lev):
-        cp = pltpu.make_async_copy(ctrl.at[0, l], S.at[:, l], loc_sem.at[3 + l])
+        cp = pltpu.make_async_copy(ctrl.at[0, l], S.at[:, l], loc_sem.at[5 + l])
         cp.start()
         ctrl_cps.append(cp)
 
+    left = lax.broadcasted_iota(jnp.int32, (hy, hy), 0)
+    right = lax.broadcasted_iota(jnp.int32, (hy, hy), 1)
+    spread[...] = jnp.where(left == (right % LANES) * parts + right // LANES, 1.0, 0.0).astype(BF16)
+    gather[...] = jnp.where(right == (left % LANES) * parts + left // LANES, 1.0, 0.0).astype(BF16)
+
     pert_cp.wait()
 
     def repack(q, carry):
-        at = pl.ds(pl.multiple_of(q * LANES, LANES), LANES)
+        at = pl.ds(pl.multiple_of(q * hy, LANES), hy)
         vals = [pert[v, :, at].astype(F32) for v in range(nvar)]
         for m in range(nm):
             piece = jnp.concatenate([v[m * lm:(m + 1) * lm] for v in vals], axis=0)
             PS[m, :, at] = piece.astype(BF16)
         return carry
 
-    lax.fori_loop(0, cols // LANES, repack, 0)
+    lax.fori_loop(0, cols // hy, repack, 0)
     pl.semaphore_wait(barrier, nm - 1 + ng - 1)
 
     def exchange(src, dst, send, recv, axis, me, d, n):
@@ -66,52 +76,63 @@
         cp.start()
 
     kidx_cp.wait()
-    index = kidx[...]
+    table_cp.wait()
+    index = jnp.dot(kidx[...].astype(F32).astype(BF16), spread[...], preferred_element_type=F32)
     field = jnp.zeros(index.shape, F32)
     for entry in range(table.shape[0]):
-        field = jnp.where(index == entry, table[entry], field)
-    kf[...] = field
-    inner = lax.broadcasted_iota(jnp.int32, (1, hy), 1) < hy - 1
-
-    def weights(i, carry):
-        own = kf[pl.ds(i, 1), :]
-        after = kf[pl.ds(jnp.minimum(i + 1, hx - 1), 1), :]
-        WE[i] = jnp.broadcast_to(0.5 * (own + after), (lev, hy))
-        north = jnp.where(inner, 0.5 * (own + pltpu.roll(own, hy - 1, axis=1)), 0.0)
-        WN[i] = jnp.broadcast_to(north, (lev, hy))
-        return carry
-
-    lax.fori_loop(0, hx, weights, 0)
-
-    def sweep(write):
-        s, before = S[0], None
-        for i in range(hx):
-            fn = WN[i] * (pltpu.roll(s, hy - 1, axis=1) - s)
-            new = s + (fn - pltpu.roll(fn, 1, axis=1))
-            if before is not None:
-                new = new - before
-            if i < hx - 1:
-                after = S[i + 1]
-                before = WE[i] * (after - s)
-                new = new + before
-                s = after
-            write(i, new)
-
-    def keep(i, new):
-        S[i] = new
-
-    def narrow(i, new):
-        B[i] = new.astype(BF16)
+        field = jnp.where(index == float(entry), table[entry], field)
+    kf[0:hx] = field
+    kf[hx:] = jnp.zeros((kf.shape[0] - hx, hy), F32)
+    east = 0.5 * (field + kf[1:hx + 1])
+    lane = lax.broadcasted_iota(jnp.int32, (hx, LANES), 1)
+    cut = [field[:, p * LANES:(p + 1) * LANES] for p in range(parts)]
+    norths = [0.5 * (cut[p] + cut[p + 1]) for p in range(parts - 1)]
+    last = 0.5 * (cut[-1] + pltpu.roll(cut[0], LANES - 1, axis=1))
+    norths.append(jnp.where(lane < LANES - 1, last, 0.0))
+    south = pltpu.roll(norths[-1], 1, axis=1)
+    for i in range(hx):
+        if i < hx - 1:
+            WE[i] = jnp.broadcast_to(east[i:i + 1], (lev, hy))
+        for p in range(parts):
+            WN[i, :, p * LANES:(p + 1) * LANES] = jnp.broadcast_to(norths[p][i:i + 1], (lev, LANES))
+        WS[i] = jnp.broadcast_to(south[i:i + 1], (lev, LANES))
 
     for cp in ctrl_cps:
         cp.wait()
+    group = rows if (rows * lev) % 8 == 0 else hx
+    for i in range(0, hx, group):
+        x = S[i:i + group].reshape(group * lev, hy)
+        high = x.astype(BF16)
+        low = (x - high.astype(F32)).astype(BF16)
+        x = (jnp.dot(high, spread[...], preferred_element_type=F32)
+             + jnp.dot(low, spread[...], preferred_element_type=F32))
+        S[i:i + group] = x.reshape(group, lev, hy)
 
     def step(it, carry):
-        sweep(keep)
-        return carry
-
-    lax.fori_loop(0, ITERS - 1, step, 0)
-    sweep(narrow)
+        s = [S[0, :, p * LANES:(p + 1) * LANES] for p in range(parts)]
+        before = None
+        for i in range(hx):
+            wn = [WN[i, :, p * LANES:(p + 1) * LANES] for p in range(parts)]
+            ahead = s[1:] + [pltpu.roll(s[0], LANES - 1, axis=1)]
+            flux = [wn[p] * (ahead[p] - s[p]) for p in range(parts)]
+            behind = [WS[i] * (s[0] - pltpu.roll(s[-1], 1, axis=1))] + flux[:-1]
+            new = [s[p] + (flux[p] - behind[p]) for p in range(parts)]
+            if before is not None:
+                new = [new[p] - before[p] for p in range(parts)]
+            if i < hx - 1:
+                after = [S[i + 1, :, p * LANES:(p + 1) * LANES] for p in range(parts)]
+                before = [WE[i, :, p * LANES:(p + 1) * LANES] * (after[p] - s[p]) for p in range(parts)]
+                new = [new[p] + before[p] for p in range(parts)]
+                s = after
+            for p in range(parts):
+                S[i, :, p * LANES:(p + 1) * LANES] = new[p]
+        return carry
+
+    lax.fori_loop(0, ITERS, step, 0)
+    for i in range(0, hx, group):
+        x = S[i:i + group].reshape(group * lev, hy).astype(BF16)
+        x = jnp.dot(x, gather[...], preferred_element_type=F32)
+        B[i:i + group] = x.reshape(group, lev, hy).astype(BF16)
 
     geo_ex = [exchange(lambda p: B.at[pl.ds(p * rows, rows)], G.at[geo], gs_sem, gr_sem, "geo", geo, d, ng)
               for d in range(1, ng)]
@@ -121,11 +142,12 @@
     own_geo.start()
 
     bands_cp.wait()
+    bounds_cp.wait()
     eye = (lax.broadcasted_iota(jnp.int32, (levels, levels), 0)
            == lax.broadcasted_iota(jnp.int32, (levels, levels), 1))
     for t in range(tiles):
         for k in range(nband):
-            row = jnp.broadcast_to(bands[t, k:k + 1, :], (levels, levels))
+            row = jnp.broadcast_to(bands[k, t:t + 1, :], (levels, levels))
             column = jnp.sum(jnp.where(eye, row, 0.0), axis=1, keepdims=True)
             bandsb[t, k] = jnp.broadcast_to(column, (levels, LANES))
 
@@ -153,7 +175,7 @@
             D[base + g * lev:base + (g + 1) * lev, r * hy:(r + 1) * hy] = G[g, r].astype(F32)
 
     def vertical(q, carry):
-        at = pl.ds(pl.multiple_of(q * LANES, LANES), LANES)
+        at = pl.ds(pl.multiple_of(q * hy, LANES), hy)
         value = D[base:base + levels, at]
         for k in range(nband):
             value = value + coef[k, :, at] * D[base + k - pad:base + k - pad + levels, at]
@@ -161,7 +183,7 @@
             FS[m, :, at] = value[m * lm:(m + 1) * lm].astype(BF16)
         return carry
 
-    lax.fori_loop(0, cols // LANES, vertical, 0)
+    lax.fori_loop(0, cols // hy, vertical, 0)
     filt_ex = [exchange(lambda p: FS.at[p], FR.at[d], fs_sem, fr_sem, "mem", mem, d, nm) for d in range(1, nm)]
     for cp in filt_ex:
         cp.start()
@@ -177,8 +199,8 @@
         cp.wait_recv()
 
     def total(q, carry):
-        at = pl.ds(pl.multiple_of(q * LANES, LANES), LANES)
-        acc = jnp.zeros((nvar * lm, LANES), F32)
+        at = pl.ds(pl.multiple_of(q * hy, LANES), hy)
+        acc = jnp.zeros((nvar * lm, hy), F32)
         for m in range(nm):
             f = FR[m, :, at].astype(F32)
             acc = acc + PR[m, :, at].astype(F32) * jnp.concatenate([f] * nvar, axis=0)
@@ -186,7 +208,7 @@
             out[v, :, at] = acc[v * lm:(v + 1) * lm]
         return carry
 
-    lax.fori_loop(0, cols // LANES, total, 0)
+    lax.fori_loop(0, cols // hy, total, 0)
     for cp in pert_ex + geo_ex + filt_ex:
         cp.wait_send()
 
@@ -199,19 +221,23 @@
     tiles, nband, _ = filter_bands.shape
     dma = pltpu.SemaphoreType.DMA
     hbm = pl.BlockSpec(memory_space=pl.ANY)
-    smem = pl.BlockSpec(memory_space=pltpu.SMEM)
     return pl.pallas_call(
         functools.partial(kernel, nm, ng),
         out_shape=jax.ShapeDtypeStruct((nvar, lm, cols), F32),
-        in_specs=[hbm, smem, hbm, smem, hbm, hbm],
+        in_specs=[hbm] * 6,
         out_specs=pl.BlockSpec(memory_space=pltpu.VMEM),
         scratch_shapes=[
+            pltpu.SMEM(kappa_table.shape, F32),
+            pltpu.SMEM(tile_bounds.shape, jnp.int32),
             pltpu.VMEM((hx, lev, hy), F32),
             pltpu.VMEM((hx, lev, hy), F32),
             pltpu.VMEM((hx, lev, hy), F32),
+            pltpu.VMEM((hx, lev, LANES), F32),
+            pltpu.VMEM((hy, hy), BF16),
+            pltpu.VMEM((hy, hy), BF16),
             pltpu.VMEM((hx, hy), jnp.int32),
-            pltpu.VMEM((hx, hy), F32),
-            pltpu.VMEM((tiles, nband, levels), F32),
+            pltpu.VMEM((hx + 8, hy), F32),
+            pltpu.VMEM((nband, tiles, levels), F32),
             pltpu.VMEM((tiles, nband, levels, LANES), F32),
             pltpu.VMEM((nband, levels, cols), F32),
             pltpu.VMEM((nvar, levels, cols), BF16),
@@ -222,11 +248,11 @@
             pltpu.VMEM((levels + 16, cols), F32),
             pltpu.VMEM((nm, lm, cols), BF16),
             pltpu.VMEM((nm, lm, cols), BF16),
-            dma((3 + lev,)), dma((nm,)), dma((nm,)), dma((ng,)), dma((ng,)), dma((nm,)), dma((nm,)),
+            dma((5 + lev,)), dma((nm,)), dma((nm,)), dma((ng,)), dma((ng,)), dma((nm,)), dma((nm,)),
         ],
         compiler_params=pltpu.CompilerParams(
             collective_id=0, has_side_effects=True, vmem_limit_bytes=56 * 2**20),
-    )(control, kappa_table, kappa_index, tile_bounds, filter_bands, perturbation)
+    )(control, kappa_table, kappa_index, tile_bounds, jnp.swapaxes(filter_bands, 0, 1), perturbation)
 
 
 def solution(mesh):

time: 48.3 us -> 28 us (0.58)
  Pallas kernels: 45.2 us -> 26.2 us
  local copies, waits for them, and re-layouts: 2.89 us -> 1.58 us
    pallas_call x1, Pallas kernels: 45.2 us -> 26.2 us  [body(): pl.pallas_call(functools.partial(kernel, nm, ng), out_shape=jax.ShapeDtyp...]
    unnamed x2 -> x1, local copies, waits for them, and re-layouts: 2.89 us -> 1.58 us
where the time goes in v2:
time: 28 us; the launch traced here: 27.8 us
  Pallas kernels  26.2 us (94%)
  local copies, waits for them, and re-layouts  1.58 us (6%)
    pallas_call x1, Pallas kernels, body(): pl.pallas_call(functools.partial(kernel, nm, ng), out_shape=jax.ShapeDtyp...  26.2 us
    unnamed x1, local copies, waits for them, and re-layouts  1.58 us

profile of v2, /device:TPU:0, one launch (start us, length us, event | category | flops | bytes accessed | tf_op | source)
XLA Modules:
  0.0 27.8 jit_solution(11061578118097716904)
XLA Ops:
  0.0 26.2 %shard_map.64 = f32[2,4,4608]{2,1,0:T(4,128)} custom-call(f32[1,8,48,384]{3,2,1,0:T(8,128)} %ctrl.1, f32[16]{0:T(128)} %table_hbm.1, s32[48,384]{1,0:T(8,128)} %kidx_hbm.1, s32[5]{0:T(128)} %bounds_hbm.1, f32[5,4,32]{2,1,0:T(4,128)} %bitcast.1, bf16[2,1,32,4608]{3,2,1,0:T(8,128)(2,1)} %pert_hbm.1), custom_call_target="tpu_custom_call" | custom-call | tf_op jit(solution)/shard_map/pallas_call | solution.py:224
  26.2 1.6 %copy.8 = f32[2,4,4608]{2,1,0:T(4,128)} copy(f32[2,4,4608]{2,1,0:T(4,128)} %shard_map.64) | data formatting | bytes 294912

commit v3 on v2

--- a/solution.py
+++ b/solution.py
@@ -13,8 +13,8 @@
 
 
 def kernel(nm, ng, ctrl, table_hbm, kidx_hbm, bounds_hbm, bands_hbm, pert_hbm, out,
-           table, bounds, S, WE, WN, WS, spread, gather, kidx, kf, bands, bandsb, coef, pert, PS, PR, B, G, D, FS, FR,
-           loc_sem, ps_sem, pr_sem, gs_sem, gr_sem, fs_sem, fr_sem):
+           table, bounds, S, WE, WN, WS, spread, gather, kidx, kf, bands, bandsb, coef, pert, PS, PR, B, G, D, FS, FR, XS, XR,
+           loc_sem, ps_sem, pr_sem, gs_sem, gr_sem, fs_sem, fr_sem, xs_sem, xr_sem):
     mem = lax.axis_index("mem")
     geo = lax.axis_index("geo")
     hx, lev, hy = S.shape
@@ -23,6 +23,7 @@
     rows = hx // ng
     nband, tiles, _ = bands.shape
     parts = hy // LANES
+    head = FS.shape[2]
     pad = nband // 2
 
     barrier = pltpu.get_barrier_semaphore()
@@ -62,7 +63,7 @@
             PS[m, :, at] = piece.astype(BF16)
         return carry
 
-    lax.fori_loop(0, cols // hy, repack, 0)
+    lax.fori_loop(0, head // hy, repack, 0)
     pl.semaphore_wait(barrier, nm - 1 + ng - 1)
 
     def exchange(src, dst, send, recv, axis, me, d, n):
@@ -174,25 +175,45 @@
         for r in range(rows):
             D[base + g * lev:base + (g + 1) * lev, r * hy:(r + 1) * hy] = G[g, r].astype(F32)
 
-    def vertical(q, carry):
+    def filtered(q):
         at = pl.ds(pl.multiple_of(q * hy, LANES), hy)
         value = D[base:base + levels, at]
         for k in range(nband):
             value = value + coef[k, :, at] * D[base + k - pad:base + k - pad + levels, at]
+        return value.astype(BF16), at
+
+    def vertical(q, carry):
+        value, at = filtered(q)
+        value = value.astype(F32)
         for m in range(nm):
             FS[m, :, at] = value[m * lm:(m + 1) * lm].astype(BF16)
         return carry
 
-    lax.fori_loop(0, cols // hy, vertical, 0)
+    lax.fori_loop(0, head // hy, vertical, 0)
     filt_ex = [exchange(lambda p: FS.at[p], FR.at[d], fs_sem, fr_sem, "mem", mem, d, nm) for d in range(1, nm)]
     for cp in filt_ex:
         cp.start()
-    own_filt = pltpu.make_async_copy(FS.at[mem], FR.at[0], fr_sem.at[0])
-    own_filt.start()
-    own_pert = pltpu.make_async_copy(PS.at[mem], PR.at[0], pr_sem.at[0])
-    own_pert.start()
-    own_pert.wait()
-    own_filt.wait()
+
+    def products(q, carry):
+        value, at = filtered(q)
+        to = pl.ds(pl.multiple_of(q * hy - head, LANES), hy)
+        vals = [pert[v, :, at].astype(F32) * value.astype(F32) for v in range(nvar)]
+        for m in range(nm):
+            piece = jnp.concatenate([v[m * lm:(m + 1) * lm] for v in vals], axis=0)
+            XS[m, :, to] = piece.astype(BF16)
+        return carry
+
+    lax.fori_loop(head // hy, cols // hy, products, 0)
+    prod_ex = [exchange(lambda p: XS.at[p], XR.at[d], xs_sem, xr_sem, "mem", mem, d, nm) for d in range(1, nm)]
+    for cp in prod_ex:
+        cp.start()
+    own = [pltpu.make_async_copy(PS.at[mem], PR.at[0], pr_sem.at[0]),
+           pltpu.make_async_copy(FS.at[mem], FR.at[0], fr_sem.at[0]),
+           pltpu.make_async_copy(XS.at[mem], XR.at[0], xr_sem.at[0])]
+    for cp in own:
+        cp.start()
+    for cp in own:
+        cp.wait()
     for cp in pert_ex:
         cp.wait_recv()
     for cp in filt_ex:
@@ -208,8 +229,21 @@
             out[v, :, at] = acc[v * lm:(v + 1) * lm]
         return carry
 
-    lax.fori_loop(0, cols // hy, total, 0)
-    for cp in pert_ex + geo_ex + filt_ex:
+    lax.fori_loop(0, head // hy, total, 0)
+    for cp in prod_ex:
+        cp.wait_recv()
+
+    def total_products(q, carry):
+        at = pl.ds(pl.multiple_of(q * hy, LANES), hy)
+        acc = XR[0, :, pl.ds(pl.multiple_of(q * hy - head, LANES), hy)].astype(F32)
+        for m in range(1, nm):
+            acc = acc + XR[m, :, pl.ds(pl.multiple_of(q * hy - head, LANES), hy)].astype(F32)
+        for v in range(nvar):
+            out[v, :, at] = acc[v * lm:(v + 1) * lm]
+        return carry
+
+    lax.fori_loop(head // hy, cols // hy, total_products, 0)
+    for cp in pert_ex + geo_ex + filt_ex + prod_ex:
         cp.wait_send()
 
 
@@ -219,6 +253,7 @@
     lm = levels // nm
     rows = hx // ng
     tiles, nband, _ = filter_bands.shape
+    head = cols - max(1, rows // 4) * hy
     dma = pltpu.SemaphoreType.DMA
     hbm = pl.BlockSpec(memory_space=pl.ANY)
     return pl.pallas_call(
@@ -241,14 +276,17 @@
             pltpu.VMEM((tiles, nband, levels, LANES), F32),
             pltpu.VMEM((nband, levels, cols), F32),
             pltpu.VMEM((nvar, levels, cols), BF16),
-            pltpu.VMEM((nm, nvar * lm, cols), BF16),
-            pltpu.VMEM((nm, nvar * lm, cols), BF16),
+            pltpu.VMEM((nm, nvar * lm, head), BF16),
+            pltpu.VMEM((nm, nvar * lm, head), BF16),
             pltpu.VMEM((hx, lev, hy), BF16),
             pltpu.VMEM((ng, rows, lev, hy), BF16),
             pltpu.VMEM((levels + 16, cols), F32),
-            pltpu.VMEM((nm, lm, cols), BF16),
-            pltpu.VMEM((nm, lm, cols), BF16),
+            pltpu.VMEM((nm, lm, head), BF16),
+            pltpu.VMEM((nm, lm, head), BF16),
+            pltpu.VMEM((nm, nvar * lm, cols - head), BF16),
+            pltpu.VMEM((nm, nvar * lm, cols - head), BF16),
             dma((5 + lev,)), dma((nm,)), dma((nm,)), dma((ng,)), dma((ng,)), dma((nm,)), dma((nm,)),
+            dma((nm,)), dma((nm,)),
         ],
         compiler_params=pltpu.CompilerParams(
             collective_id=0, has_side_effects=True, vmem_limit_bytes=56 * 2**20),

time: 28 us -> 27.4 us (0.979)
  Pallas kernels: 26.2 us -> 25.7 us
    pallas_call x1, Pallas kernels: 26.2 us -> 25.7 us  [body(): pl.pallas_call(functools.partial(kernel, nm, ng), out_shape=jax.ShapeDtyp...]
where the time goes in v3:
time: 27.4 us; the launch traced here: 27.3 us
  Pallas kernels  25.7 us (94%)
  local copies, waits for them, and re-layouts  1.58 us (6%)
    pallas_call x1, Pallas kernels, body(): pl.pallas_call(functools.partial(kernel, nm, ng), out_shape=jax.ShapeDtyp...  25.7 us
    unnamed x1, local copies, waits for them, and re-layouts  1.58 us

profile of v3, /device:TPU:0, one launch (start us, length us, event | category | flops | bytes accessed | tf_op | source)
XLA Modules:
  0.0 27.3 jit_solution(15715281951353209560)
XLA Ops:
  0.0 25.7 %shard_map.64 = f32[2,4,4608]{2,1,0:T(4,128)} custom-call(f32[1,8,48,384]{3,2,1,0:T(8,128)} %ctrl.1, f32[16]{0:T(128)} %table_hbm.1, s32[48,384]{1,0:T(8,128)} %kidx_hbm.1, s32[5]{0:T(128)} %bounds_hbm.1, f32[5,4,32]{2,1,0:T(4,128)} %bitcast.1, bf16[2,1,32,4608]{3,2,1,0:T(8,128)(2,1)} %pert_hbm.1), custom_call_target="tpu_custom_call" | custom-call | tf_op jit(solution)/shard_map/pallas_call | solution.py:259
  25.7 1.6 %copy.8 = f32[2,4,4608]{2,1,0:T(4,128)} copy(f32[2,4,4608]{2,1,0:T(4,128)} %shard_map.64) | data formatting | bytes 294912

commit v4 on v3

--- a/solution.py
+++ b/solution.py
@@ -26,6 +26,7 @@
     head = FS.shape[2]
     pad = nband // 2
 
+    far_first = sorted(range(1, nm), key=lambda d: abs(2 * d - nm))
     barrier = pltpu.get_barrier_semaphore()
     for d in range(1, nm):
         pl.semaphore_signal(barrier, inc=1, device_id={"mem": lax.rem(mem + d, nm)}, device_id_type=pl.DeviceIdType.MESH)
@@ -72,7 +73,7 @@
             src_ref=src(peer), dst_ref=dst, send_sem=send.at[d], recv_sem=recv.at[d],
             device_id={axis: peer}, device_id_type=pl.DeviceIdType.MESH)
 
-    pert_ex = [exchange(lambda p: PS.at[p], PR.at[d], ps_sem, pr_sem, "mem", mem, d, nm) for d in range(1, nm)]
+    pert_ex = [exchange(lambda p: PS.at[p], PR.at[d], ps_sem, pr_sem, "mem", mem, d, nm) for d in far_first]
     for cp in pert_ex:
         cp.start()
 
@@ -190,7 +191,7 @@
         return carry
 
     lax.fori_loop(0, head // hy, vertical, 0)
-    filt_ex = [exchange(lambda p: FS.at[p], FR.at[d], fs_sem, fr_sem, "mem", mem, d, nm) for d in range(1, nm)]
+    filt_ex = [exchange(lambda p: FS.at[p], FR.at[d], fs_sem, fr_sem, "mem", mem, d, nm) for d in far_first]
     for cp in filt_ex:
         cp.start()
 
@@ -204,7 +205,7 @@
         return carry
 
     lax.fori_loop(head // hy, cols // hy, products, 0)
-    prod_ex = [exchange(lambda p: XS.at[p], XR.at[d], xs_sem, xr_sem, "mem", mem, d, nm) for d in range(1, nm)]
+    prod_ex = [exchange(lambda p: XS.at[p], XR.at[d], xs_sem, xr_sem, "mem", mem, d, nm) for d in far_first]
     for cp in prod_ex:
         cp.start()
     own = [pltpu.make_async_copy(PS.at[mem], PR.at[0], pr_sem.at[0]),

time: 27.4 us -> 27.6 us (level)
  no operation moved by 1% of the time
where the time goes in v4:
time: 27.6 us; the launch traced here: 27.5 us
  Pallas kernels  25.9 us (94%)
  local copies, waits for them, and re-layouts  1.58 us (6%)
    pallas_call x1, Pallas kernels, body(): pl.pallas_call(functools.partial(kernel, nm, ng), out_shape=jax.ShapeDtyp...  25.9 us
    unnamed x1, local copies, waits for them, and re-layouts  1.58 us

profile of v4, /device:TPU:0, one launch (start us, length us, event | category | flops | bytes accessed | tf_op | source)
XLA Modules:
  0.0 27.5 jit_solution(13861709876433812812)
XLA Ops:
  0.0 25.9 %shard_map.64 = f32[2,4,4608]{2,1,0:T(4,128)} custom-call(f32[1,8,48,384]{3,2,1,0:T(8,128)} %ctrl.1, f32[16]{0:T(128)} %table_hbm.1, s32[48,384]{1,0:T(8,128)} %kidx_hbm.1, s32[5]{0:T(128)} %bounds_hbm.1, f32[5,4,32]{2,1,0:T(4,128)} %bitcast.1, bf16[2,1,32,4608]{3,2,1,0:T(8,128)(2,1)} %pert_hbm.1), custom_call_target="tpu_custom_call" | custom-call | tf_op jit(solution)/shard_map/pallas_call | solution.py:260
  25.9 1.6 %copy.8 = f32[2,4,4608]{2,1,0:T(4,128)} copy(f32[2,4,4608]{2,1,0:T(4,128)} %shard_map.64) | data formatting | bytes 294912
